TPU v7x, 32 devices: a whole 2x2x4 slice. The times are simulated.
32 devices in a mesh: dp: 4 (over x, y), tp: 8 (over z, core).
Axes of the slice: x: 2, y: 2, z: 4, core: 2. Of those that a mesh axis runs over, the one named last changes fastest.
Arguments:
- x: bfloat16 [256, 3072], P('dp'), parts along dimension 0
- k_cache: bfloat16 [256, 4096, 8, 128], P('dp', None, 'tp'), parts along dimension 0
- v_cache: bfloat16 [256, 4096, 8, 128], P('dp', None, 'tp'), parts along dimension 0
- gain_a: bfloat16 [3072], replicated
- wq: bfloat16 [3072, 3072], P(None, 'tp')
- wo: bfloat16 [3072, 3072], P('tp')
- gain_m: bfloat16 [3072], replicated
- w_gate: bfloat16 [3072, 8192], P(None, 'tp')
- w_up: bfloat16 [3072, 8192], P(None, 'tp')
- w_down: bfloat16 [8192, 3072], P('tp')
Outputs:
- output: bfloat16 [256, 3072], P('dp'), parts along dimension 0
There are 4 independent parts. A program takes and returns all parts, laid end to end along the dimension named above; an argument that names none is the same for every part.
All inputs are finite; a program needn't handle non-finite values.
Results may differ from a plain program's by a relative error of at most 0.017.
Values are sent between devices in bfloat16 or wider.
A program may use at most 2 GiB of HBM per device.

v0:
```python
import jax
import jax.numpy as jnp
from jax import lax
from jax.sharding import PartitionSpec as P

HEAD = 128
THETA = 10000


def normed(x, gain):
    wide = x.astype(jnp.float32)
    scale = lax.rsqrt(jnp.mean(wide * wide, -1, keepdims=True) + 1e-6)
    return (wide * scale * gain.astype(jnp.float32)).astype(jnp.bfloat16)


def turned(t, place, theta):
    half = t.shape[-1] // 2
    angle = place.astype(jnp.float32)[:, None] * theta ** (-jnp.arange(half, dtype=jnp.float32) / half)
    cos, sin = jnp.cos(angle)[:, None], jnp.sin(angle)[:, None]
    a, b = t[..., :half].astype(jnp.float32), t[..., half:].astype(jnp.float32)
    return jnp.concatenate([a * cos - b * sin, b * cos + a * sin], -1).astype(jnp.bfloat16)


def matmul(a, w):
    return jnp.dot(a, w, preferred_element_type=jnp.float32).astype(jnp.bfloat16)


def einsum(form, a, b):
    return jnp.einsum(form, a.astype(jnp.float32), b.astype(jnp.float32))


def seen_by(a, wq, k_cache, v_cache, head, theta):
    batch, cache, kv_heads = k_cache.shape[:3]
    place = jnp.full((batch,), cache - 1)
    q = turned(matmul(a, wq).reshape(batch, -1, head), place, theta).reshape(batch, kv_heads, -1, head)
    scores = einsum("bgsd,bugd->bgsu", q, k_cache) * head**-0.5
    weights = jax.nn.softmax(scores, -1).astype(jnp.bfloat16)
    return einsum("bgsu,bugd->bgsd", weights, v_cache).astype(jnp.bfloat16).reshape(batch, -1)


def hidden_of(b, w_gate, w_up):
    gate = jnp.dot(b, w_gate, preferred_element_type=jnp.float32)
    up = jnp.dot(b, w_up, preferred_element_type=jnp.float32)
    return (jax.nn.silu(gate) * up).astype(jnp.bfloat16)


def solution(mesh):
    def added(t, term):
        return (t.astype(jnp.float32) + lax.psum(term.astype(jnp.bfloat16), "tp").astype(jnp.float32)).astype(jnp.bfloat16)

    def step(x, k_cache, v_cache, gain_a, wq, wo, gain_m, w_gate, w_up, w_down):
        seen = seen_by(normed(x, gain_a), wq, k_cache, v_cache, HEAD, THETA)
        h = added(x, jnp.dot(seen, wo, preferred_element_type=jnp.float32))
        return added(h, jnp.dot(hidden_of(normed(h, gain_m), w_gate, w_up), w_down, preferred_element_type=jnp.float32))

    states, cache, columns, rows_of = P("dp", None), P("dp", None, "tp", None), P(None, "tp"), P("tp", None)
    return jax.shard_map(
        step,
        mesh=mesh,
        in_specs=(states, cache, cache, P(None), columns, rows_of, P(None), columns, columns, rows_of),
        out_specs=states,
        check_vma=False,
    )
```

profile of v0, /device:TPU:0, one launch (start us, length us, event | category | flops | bytes accessed | tf_op | source)
XLA Modules:
  0.0 199.7 jit_solution(16378961998498412219)
XLA Ops:
  6.5 0.0 copy-start
  6.5 0.0 all-reduce.3.cloned.1.call-start
  6.6 0.8 convert_element_type.66
  7.4 1.2 fusion.15
  8.6 2.4 %convolution_convert_fusion.2 = bf16[64,384]{1,0:T(8,128)(2,1)S(1)} fusion(bf16[3072,384]{1,0:T(8,128)(2,1)} %param.14, bf16[64,3072]{1,0:T(8,128)(2,1)} %param.10, f32[3072]{0:T(1024)S(1)} %convert_element_type.66, f32[64]{0:T(128)S(1)} %add_rsqrt_fusion.1), kind=kOutput, calls=%fused_computation.21 | convolution fusion | flops 151805952 | bytes 2814208 | tf_op jit(solution)/shard_map/dot_general | solution.py:25
  11.0 0.1 fusion.47
  11.2 0.1 pad_maximum_fusion
  11.3 27.7 %fusion.48 = (f32[64,3]{1,0:T(8,128)S(1)}, f32[64,3,4096]{2,1,0:T(4,128)}) fusion(bf16[64,4096,1,128]{3,1,2,0:T(8,128)(2,1)} %param.11, bf16[64,3,128]{2,0,1:T(8,128)(2,1)S(1)} %pad_maximum_fusion), kind=kOutput, calls=%fused_computation.58 | convolution fusion | flops 203689984 | bytes 70304512 | tf_op jit(solution)/shard_map/sub | solution.py:37
  39.0 0.0 copy-start.2
  39.0 0.0 copy-start.1
  39.0 24.0 %fusion.12 = bf16[64,3,128]{2,1,0:T(4,128)(2,1)S(1)} fusion(bf16[64,4096,1,128]{3,1,2,0:T(8,128)(2,1)} %param.12, f32[64,3,4096]{2,1,0:T(4,128)} %get-tuple-element.12, f32[64,3]{1,0:T(8,128)S(1)} %get-tuple-element.11), kind=kOutput, calls=%fused_computation.20 | convolution fusion | flops 202924032 | bytes 70304512 | tf_op jit(solution)/shard_map/bgsu,bugd->bgsd/dot_general | solution.py:29
  63.0 0.0 copy-done
  63.0 1.3 convolution_convert_fusion.1
  64.3 0.0 all-reduce.3.cloned.1.call-update
  64.3 0.0 all-reduce.5.cloned.1.call-start
  64.4 0.0 copy-done.2
  64.4 58.6 %all-reduce.3.cloned.1.call-done = bf16[64,3072]{1,0:T(8,128)(2,1)} async-done(((bf16[64,3072]{1,0:T(8,128)(2,1)}), bf16[64,3072]{1,0:T(8,128)(2,1)}) %all-reduce.3.cloned.1.call-update) | async-done | bytes 393232 | tf_op jit(solution)/shard_map/psum | solution.py:49
  123.0 0.0 copy-done.1
  123.0 1.2 fusion.19
  124.3 4.0 %fusion.34 = f32[64,1024]{1,0:T(8,128)S(1)} fusion(bf16[3072,1024]{1,0:T(8,128)(2,1)} %param.17, bf16[64,3072]{1,0:T(8,128)(2,1)S(1)} %get-tuple-element.6, f32[3072]{0:T(1024)S(1)} %convert_element_type.77, f32[64]{0:T(128)S(1)} %add_rsqrt_fusion), kind=kOutput, calls=%fused_computation.42 | convolution fusion | flops 403439616 | bytes 6959360 | tf_op jit(solution)/shard_map/dot_general | solution.py:42
  128.3 7.7 %convolution_convert_fusion = bf16[64,3072]{1,0:T(8,128)(2,1)} fusion(bf16[1024,3072]{1,0:T(8,128)(2,1)} %param.19, bf16[3072,1024]{1,0:T(8,128)(2,1)} %param.18, f32[64,1024]{1,0:T(8,128)S(1)} %fusion.34, bf16[64,3072]{1,0:T(8,128)(2,1)S(1)} %get-tuple-element.6, f32[3072]{0:T(1024)S(1)} %convert_element_type.77, f32[64]{0:T(128)S(1)} %add_rsqrt_fusion), kind=kOutput, calls=%fused_computation.9 | convolution fusion | flops 806682624 | bytes 13644032 | tf_op jit(solution)/shard_map/dot_general | solution.py:54
  136.0 0.0 all-reduce.5.cloned.1.call-update
  136.1 55.0 %all-reduce.5.cloned.1.call-done = bf16[64,3072]{1,0:T(8,128)(2,1)} async-done(((bf16[64,3072]{1,0:T(8,128)(2,1)}), bf16[64,3072]{1,0:T(8,128)(2,1)}) %all-reduce.5.cloned.1.call-update) | async-done | bytes 393232 | tf_op jit(solution)/shard_map/psum | solution.py:49
  191.1 1.8 fusion.22
  (6 shorter events, 0.1 us)
Async XLA Ops:
  6.5 56.5 %copy-start = (bf16[384,3072]{1,0:T(8,128)(2,1)S(1)}, bf16[384,3072]{1,0:T(8,128)(2,1)}, u32[]{:S(2)}) copy-start(bf16[384,3072]{1,0:T(8,128)(2,1)} %param.15) | copy-start | bytes 7077892
  6.5 116.5 %all-reduce.3.cloned.1.call-start = ((), (), s32[]{:S(2)}) async-start(), calls=%async_computation | async-start | bytes 786432 | tf_op jit(solution)/shard_map/psum | solution.py:49
  39.0 25.4 %copy-start.2 = (bf16[3072]{0:T(1024)(128)(2,1)S(1)}, bf16[3072]{0:T(1024)(128)(2,1)}, u32[]{:S(2)}) copy-start(bf16[3072]{0:T(1024)(128)(2,1)} %param.16) | copy-start | bytes 18436
  39.0 84.0 %copy-start.1 = (bf16[64,3072]{1,0:T(8,128)(2,1)S(1)}, bf16[64,3072]{1,0:T(8,128)(2,1)}, u32[]{:S(2)}) copy-start(bf16[64,3072]{1,0:T(8,128)(2,1)} %param.10) | copy-start | bytes 1179652
  64.3 126.7 %all-reduce.5.cloned.1.call-start = ((), (), s32[]{:S(2)}) async-start(), calls=%async_computation.1 | async-start | bytes 786432 | tf_op jit(solution)/shard_map/psum | solution.py:49
Sparse Core Ops, SparseCore 0:
  64.4 58.5 all-reduce.2
  136.2 54.8 all-reduce.4
where the time goes:
time: 200 us
  waiting for transfers between devices  114 us (57%)
  matrix products  67.1 us (34%)
  between operations  13.5 us (7%)
  other arithmetic  5.28 us (3%)
    psum x2, waiting for transfers between devices, added(): lax.psum(term.astype(jnp.bfloat16), 'tp').astype(jnp.float32)  114 us
    sub x1, matrix products, seen_by(): weights = jax.nn.softmax(scores, -1).astype(jnp.bfloat16)  27.7 us
    dot_general x1, matrix products, einsum(): return jnp.einsum(form, a.astype(jnp.float32), b.astype(jnp.float32))  24 us
    dot_general x1, matrix products, step(): jnp.dot(hidden_of(normed(h, gain_m), w_gate, w_up), w_down, preferred_ele...  7.72 us
    dot_general x1, matrix products, hidden_of(): gate = jnp.dot(b, w_gate, preferred_element_type=jnp.float32)  4.05 us
  transfers between devices with their start and end apart: 2, of which 2 were waited for; matrix products, arithmetic and copies ran while one was open for 0% of the time, Pallas kernels for 0%

commit v1 on v0

v1 whole, which is shorter than its diff:
```python
import functools

import jax
import jax.numpy as jnp
import numpy as np
from jax import lax
from jax.experimental import pallas as pl
from jax.experimental.pallas import tpu as pltpu
from jax.sharding import PartitionSpec as P

HEAD = 128
THETA = 10000
SEQS, CACHE, D, FF, TP = 64, 4096, 3072, 8192, 8
QH = 3
HALF = D // 2
HID = FF // TP
SLOTS = 6
UNIT = 2
STEPS = SEQS // (2 * UNIT)
F32, BF16 = jnp.float32, jnp.bfloat16

GROUPS = (24, 16, 16, 8)
AFTER = {
    5: [("wo", 0)],
    6: [("share1", 0)],
    9: [("wo", 1)],
    10: [("share1", 1), ("h", 0)],
    11: [("mlp", 0)],
    12: [("share2", 0)],
    13: [("wo", 2)],
    14: [("share1", 2), ("h", 1)],
    15: [
        ("wo", 3), ("share1", 3), ("mlp", 1), ("share2", 1), ("y", 0), ("h", 2), ("mlp", 2), ("share2", 2), ("h", 3), ("mlp", 3),
        ("share2", 3), ("out", 0), ("y", 1), ("out", 1), ("y", 2), ("out", 2), ("y", 3), ("out", 3),
    ],
}


def rotary():
    half = HEAD // 2
    angle = np.float32(CACHE - 1) * np.float32(THETA) ** (-np.arange(half, dtype=np.float32) / np.float32(half))
    cos, sin = np.cos(angle), np.sin(angle)
    return np.concatenate([cos, cos]).astype(np.float32), np.concatenate([-sin, sin]).astype(np.float32)


def kernel(
    x_hbm, k_hbm, v_hbm, small_hbm, wq_hbm, wo_hbm, wg_hbm, wu_hbm, wd_hbm, y_hbm,
    small, wq, wo, wg, wu, wd, kbuf, vbuf, sbuf, obuf, qbuf, xs, sends, gots, mines, parts, halves,
    ksem, vsem, wsem, xsem, ysem, ssem, rsem,
):
    me = lax.axis_index("tp")
    z, c = me // 2, me % 2
    firsts = [sum(GROUPS[:g]) for g in range(len(GROUPS))]

    barrier = pltpu.get_barrier_semaphore()
    partner = 2 * z + (1 - c)
    others = [2 * lax.rem(z + d, 4) + c for d in (1, 2, 3)]
    for peer in (partner, *others):
        pl.semaphore_signal(barrier, inc=1, device_id={"tp": peer}, device_id_type=pl.DeviceIdType.MESH)

    xcopies = [
        pltpu.make_async_copy(x_hbm.at[pl.ds(firsts[g], rows), pl.ds(i * HALF, HALF)], xs[g].at[i], xsem.at[g, i])
        for g, rows in enumerate(GROUPS)
        for i in range(2)
    ]
    small_copy = pltpu.make_async_copy(small_hbm, small, wsem.at[0])
    wcopies = [
        pltpu.make_async_copy(source, target, wsem.at[1 + i])
        for i, (source, target) in enumerate([(wq_hbm, wq), (wo_hbm, wo), (wg_hbm, wg), (wu_hbm, wu), (wd_hbm, wd)])
    ]

    def kcopy(p):
        slot = lax.rem(p, SLOTS)
        return pltpu.make_async_copy(k_hbm.at[pl.ds(2 * p, 2)], kbuf.at[slot], ksem.at[slot])

    def vcopy(p):
        slot = lax.rem(p, SLOTS)
        return pltpu.make_async_copy(v_hbm.at[pl.ds(2 * p, 2)], vbuf.at[slot], vsem.at[slot])

    for copy in (*xcopies, small_copy, wcopies[0]):
        copy.start()
    for p in range(SLOTS):
        kcopy(p).start()
        vcopy(p).start()
    for copy in wcopies[1:]:
        copy.start()

    def normed(wide, gain):
        scale = lax.rsqrt(jnp.mean(wide * wide, -1, keepdims=True) + 1e-6)
        return (wide * scale * gain).astype(BF16)

    for copy in (*xcopies, small_copy, wcopies[0]):
        copy.wait()
    wide = jnp.concatenate([jnp.concatenate([x[0].astype(F32), x[1].astype(F32)], 1) for x in xs], 0)
    q = jnp.dot(normed(wide, small[0:1, :]), wq[...], preferred_element_type=F32).astype(BF16).astype(F32)
    cos, sin = small[2:3, 0:HEAD], small[3:4, 0:HEAD]
    qbuf[...] = jnp.zeros_like(qbuf)
    for s in range(QH):
        t = q[:, s * HEAD : (s + 1) * HEAD]
        turned = t * cos + pltpu.roll(t, HEAD // 2, 1) * sin
        qbuf[:, s, :] = turned.astype(BF16).astype(F32)

    tile = 256

    def scores(p):
        slot, kept = lax.rem(p, SLOTS), lax.rem(p, 2 * UNIT)
        first = qbuf[2 * p]
        second = pltpu.roll(qbuf[2 * p + 1], QH, 0)
        row = lax.broadcasted_iota(jnp.int32, first.shape, 0)
        second = jnp.where((row >= QH) & (row < 2 * QH), second, 0.0)
        both = jnp.concatenate([first, second], 1).astype(BF16)
        for i in range(CACHE // tile):
            at = pl.ds(i * tile, tile)
            keys = jnp.concatenate([kbuf[slot, 0, at, :], kbuf[slot, 1, at, :]], 1)
            found = lax.dot_general(both, keys, (((1,), (1,)), ((), ())), preferred_element_type=F32)
            sbuf[kept, :, at] = found * HEAD**-0.5

    def finish(p):
        slot, kept = lax.rem(p, SLOTS), lax.rem(p, 2 * UNIT)
        s = sbuf[kept]
        e = jnp.exp(s - jnp.max(s, -1, keepdims=True))
        w = (e * (1.0 / jnp.sum(e, -1, keepdims=True))).astype(BF16)
        sums = [None, None]
        for i in range(CACHE // tile):
            at = pl.ds(i * tile, tile)
            values = jnp.concatenate([vbuf[slot, 0, at, :], vbuf[slot, 1, at, :]], 1)
            term = jnp.dot(w[:, i * tile : (i + 1) * tile], values, preferred_element_type=F32)
            sums[i % 2] = term if sums[i % 2] is None else sums[i % 2] + term
        for i, total in enumerate(sums):
            obuf[i, pl.ds(pl.multiple_of(16 * p, 16), 8), :] = total[:, :HEAD]
            obuf[i, pl.ds(pl.multiple_of(16 * p + 8, 8), 8), :] = pltpu.roll(total[:, HEAD:], 8 - QH, 0)

    def step(k, last):
        for u in range(UNIT):
            vcopy(k * UNIT + u).wait()
            if not last:
                kcopy((k + 1) * UNIT + u).wait()
        for u in range(UNIT):
            finish(k * UNIT + u)
        if last:
            return
        for u in range(UNIT):
            scores((k + 1) * UNIT + u)
        for u in range(UNIT):
            for copy, p in ((vcopy, k * UNIT + u), (kcopy, (k + 1) * UNIT + u)):

                @pl.when(p + SLOTS < SEQS // 2)
                def _():
                    copy(p + SLOTS).start()

    def remote(n, g, i, source, target, peer):
        return pltpu.make_async_remote_copy(
            src_ref=source,
            dst_ref=target,
            send_sem=ssem.at[n, g, i],
            recv_sem=rsem.at[n, g, i],
            device_id={"tp": peer},
            device_id_type=pl.DeviceIdType.MESH,
        )

    def to_partner(n, g):
        return remote(n, g, 0, sends[n][g], gots[n][g], partner)

    def to_others(n, g):
        return [remote(n, g, d, parts[n][g].at[0], parts[n][g].at[d], others[d - 1]) for d in (1, 2, 3)]

    def halves_to_partner(n, g):
        return remote(n, g, 4, halves[n][g].at[c], halves[n][g].at[c], partner)

    def terms(n, g, left, right_ref):
        width = 512
        for mine in (False, True):
            base = (c if mine else 1 - c) * HALF
            for j in range(HALF // width):
                at = pl.ds(pl.multiple_of(base + j * width, width), width)
                term = jnp.dot(left, right_ref[:, at], preferred_element_type=F32)
                if mine:
                    mines[n][g][:, j * width : (j + 1) * width] = term
                else:
                    sends[n][g][:, j * width : (j + 1) * width] = term.astype(BF16)
            if not mine:
                to_partner(n, g).start()

    def share(n, g):
        to_partner(n, g).wait()
        parts[n][g][0] = (mines[n][g][...] + gots[n][g][...].astype(F32)).astype(BF16)
        for copy in to_others(n, g):
            copy.start()

    def summed(n, g, base):
        for copy in to_others(n, g):
            copy.wait()
        total = None
        for chip in range(4):
            part = parts[n][g][lax.rem(z - chip + 4, 4)].astype(F32)
            total = part if total is None else total + part
        halves[n][g][c] = (base.astype(F32) + total).astype(BF16)
        halves_to_partner(n, g).start()

    started = set()

    def do(what, g):
        rows = GROUPS[g]
        if what == "wo":
            if not started:
                pl.semaphore_wait(barrier, 4)
                wcopies[1].wait()
            started.add("wo")
            seen = []
            for s in range(QH):
                at = pl.ds(8 * firsts[g] + s, rows, stride=8)
                seen.append(obuf[0, at, :] + obuf[1, at, :])
            terms(0, g, jnp.concatenate(seen, 1).astype(BF16), wo)
        elif what == "share1":
            share(0, g)
        elif what == "h":
            summed(0, g, xs[g][c])
        elif what == "mlp":
            if "mlp" not in started:
                for copy in wcopies[2:]:
                    copy.wait()
            started.add("mlp")
            halves_to_partner(0, g).wait()
            h = jnp.concatenate([halves[0][g][0].astype(F32), halves[0][g][1].astype(F32)], 1)
            b = normed(h, small[1:2, :])
            hidden = []
            for j in range(HID // tile):
                at = pl.ds(j * tile, tile)
                gate = jnp.dot(b, wg[:, at], preferred_element_type=F32)
                up = jnp.dot(b, wu[:, at], preferred_element_type=F32)
                hidden.append((jax.nn.silu(gate) * up).astype(BF16))
            terms(1, g, jnp.concatenate(hidden, 1), wd)
        elif what == "share2":
            share(1, g)
        elif what == "y":
            summed(1, g, halves[0][g][c])
        elif what == "out":
            halves_to_partner(1, g).wait()
            for i in range(2):
                ycopy(g, i).start()

    def ycopy(g, i):
        return pltpu.make_async_copy(halves[1][g].at[i], y_hbm.at[pl.ds(firsts[g], GROUPS[g]), pl.ds(i * HALF, HALF)], ysem.at[g, i])

    for u in range(UNIT):
        kcopy(u).wait()
        scores(u)
        kcopy(u + SLOTS).start()
    at = 0
    for k in sorted(AFTER):
        if k < STEPS - 1:
            lax.fori_loop(at, k + 1, lambda i, _: step(i, False), None)
        else:
            if at < STEPS - 1:
                lax.fori_loop(at, STEPS - 1, lambda i, _: step(i, False), None)
            step(STEPS - 1, True)
        at = k + 1
        for what, g in AFTER[k]:
            do(what, g)
    for g in range(len(GROUPS)):
        for i in range(2):
            ycopy(g, i).wait()


def layer(x, k, v, small, wq, wo, wg, wu, wd):
    n = len(GROUPS)
    per_group = lambda *shape, dtype=BF16, lead=(): [pltpu.VMEM((*lead, rows, *shape), dtype) for rows in GROUPS]
    return pl.pallas_call(
        kernel,
        out_shape=jax.ShapeDtypeStruct((SEQS, D), BF16),
        in_specs=[pl.BlockSpec(memory_space=pltpu.HBM)] * 9,
        out_specs=pl.BlockSpec(memory_space=pltpu.HBM),
        scratch_shapes=[
            pltpu.VMEM(small.shape, F32),
            pltpu.VMEM(wq.shape, BF16),
            pltpu.VMEM(wo.shape, BF16),
            pltpu.VMEM(wg.shape, BF16),
            pltpu.VMEM(wu.shape, BF16),
            pltpu.VMEM(wd.shape, BF16),
            pltpu.VMEM((SLOTS, 2, CACHE, HEAD), BF16),
            pltpu.VMEM((SLOTS, 2, CACHE, HEAD), BF16),
            pltpu.VMEM((2 * UNIT, 8, CACHE), F32),
            pltpu.VMEM((2, SEQS * 8, HEAD), F32),
            pltpu.VMEM((SEQS, 8, HEAD), F32),
            per_group(HALF, lead=(2,)),
            [per_group(HALF), per_group(HALF)],
            [per_group(HALF), per_group(HALF)],
            [per_group(HALF, dtype=F32), per_group(HALF, dtype=F32)],
            [per_group(HALF, lead=(4,)), per_group(HALF, lead=(4,))],
            [per_group(HALF, lead=(2,)), per_group(HALF, lead=(2,))],
            pltpu.SemaphoreType.DMA((SLOTS,)),
            pltpu.SemaphoreType.DMA((SLOTS,)),
            pltpu.SemaphoreType.DMA((6,)),
            pltpu.SemaphoreType.DMA((n, 2)),
            pltpu.SemaphoreType.DMA((n, 2)),
            pltpu.SemaphoreType.DMA((2, n, 5)),
            pltpu.SemaphoreType.DMA((2, n, 5)),
        ],
        compiler_params=pltpu.CompilerParams(collective_id=0, has_side_effects=True, vmem_limit_bytes=63 * 2**20),
    )(x, k, v, small, wq, wo, wg, wu, wd)


def solution(mesh):
    cos, sin = rotary()

    def step(x, k_cache, v_cache, gain_a, wq, wo, gain_m, w_gate, w_up, w_down):
        seqs, cache = k_cache.shape[:2]
        pad = lambda t: np.concatenate([t, np.zeros(D - HEAD, np.float32)])
        small = jnp.stack([gain_a.astype(F32), gain_m.astype(F32), pad(cos), pad(sin)])
        return layer(
            x, k_cache.reshape(seqs, cache, HEAD), v_cache.reshape(seqs, cache, HEAD), small, wq, wo, w_gate, w_up, w_down
        )

    states, cache, columns, rows_of = P("dp", None), P("dp", None, "tp", None), P(None, "tp"), P("tp", None)
    return jax.shard_map(
        step,
        mesh=mesh,
        in_specs=(states, cache, cache, P(None), columns, rows_of, P(None), columns, columns, rows_of),
        out_specs=states,
        check_vma=False,
    )
```

time: 200 us -> 84.2 us (0.42)
  waiting for transfers between devices: 114 us -> 0 us
  Pallas kernels: 0 us -> 79.3 us
  matrix products: 67.1 us -> 0 us
  between operations: 13.5 us -> 0.01 us
  other arithmetic: 5.28 us -> 2.78 us
    psum x2 -> x0, waiting for transfers between devices: 114 us -> none  [added(): lax.psum(term.astype(jnp.bfloat16), 'tp').astype(jnp.float32)]
    pallas_call x0 -> x1, Pallas kernels: none -> 79.3 us  [layer(): pl.pallas_call(kernel, out_shape=jax.ShapeDtypeStruct((SEQS, D), BF16), i...]
    dot_general x5 -> x0, matrix products: 39.4 us -> none  [the longest x1 24 us: einsum(): return jnp.einsum(form, a.astype(jnp.float32), b.astype(jnp.float32))]
    sub x1 -> x0, matrix products: 27.7 us -> none  [seen_by(): weights = jax.nn.softmax(scores, -1).astype(jnp.bfloat16)]
    another operation x1 -> x3, other arithmetic: 0.04 us -> 2.78 us  [step(): jnp.stack([gain_a.astype(F32), gain_m.astype(F32), pad(cos), pad(sin)])]
    convert_element_type x3 -> x0, other arithmetic: 2.69 us -> none  [the longest x1 1.83 us: added(): (t.astype(jnp.float32) + lax.psum(term.astype(jnp.bfloat16), 'tp').astype...]
    reduce_sum x2 -> x0, other arithmetic: 2.41 us -> none  [normed(): scale = lax.rsqrt(jnp.mean(wide * wide, -1, keepdims=True) + 1e-06)]
  transfers between devices with their start and end apart: 2 -> 0, of which waited for: 2 -> 0; matrix products, arithmetic and copies ran while one was open for 0% -> 0% of each run, Pallas kernels for 0% -> 0%
where the time goes in v1:
time: 84.2 us; the launch traced here: 83.8 us
  Pallas kernels  79.3 us (94%)
  other arithmetic  2.78 us (3%)
  local copies, waits for them, and re-layouts  1.77 us (2%)
    pallas_call x1, Pallas kernels, layer(): pl.pallas_call(kernel, out_shape=jax.ShapeDtypeStruct((SEQS, D), BF16), i...  79.3 us
    another operation x3, other arithmetic, step(): jnp.stack([gain_a.astype(F32), gain_m.astype(F32), pad(cos), pad(sin)])  2.78 us
    unnamed x1, local copies, waits for them, and re-layouts  1.77 us

profile of v1, /device:TPU:0, one launch (start us, length us, event | category | flops | bytes accessed | tf_op | source)
XLA Modules:
  0.0 83.8 jit_solution(14258441632694339734)
XLA Ops:
  0.0 0.7 stack.28
  0.7 0.7 stack.29
  1.4 1.4 %pad_maximum_fusion.small_hbm = f32[4,3072]{1,0:T(4,128)} fusion(f32[1,3072]{1,0:T(1,128)} %constant.9, f32[1,3072]{1,0:T(1,128)} %constant.8, f32[1,3072]{1,0:T(1,128)S(1)} %bitcast.5, f32[1,3072]{1,0:T(1,128)S(1)} %bitcast.4), kind=kLoop, calls=%fused_computation | loop fusion | flops 36864 | bytes 98304 | tf_op jit(solution)/shard_map/stack | solution.py:309
  2.8 79.3 %shard_map.118 = bf16[64,3072]{1,0:T(8,128)(2,1)} custom-call(bf16[64,3072]{1,0:T(8,128)(2,1)} %x_hbm.1, bf16[64,4096,128]{2,1,0:T(8,128)(2,1)} %bitcast.k_hbm, bf16[64,4096,128]{2,1,0:T(8,128)(2,1)} %bitcast.1.v_hbm, f32[4,3072]{1,0:T(4,128)} %pad_maximum_fusion.small_hbm, bf16[3072,384]{1,0:T(8,128)(2,1)} %wq_hbm.1, bf16[384,3072]{1,0:T(8,128)(2,1)} %wo_hbm.1, ...), custom_call_target="tpu_custom_call" | custom-call | tf_op jit(solution)/shard_map/pallas_call | solution.py:268
  82.1 1.8 %copy.14 = bf16[64,3072]{1,0:T(8,128)(2,1)} copy(bf16[64,3072]{1,0:T(8,128)(2,1)} %shard_map.118) | data formatting | bytes 786432

commit v2 on v1

v2 whole, which is shorter than its diff:
```python
import jax
import jax.numpy as jnp
import numpy as np
from jax import lax
from jax.experimental import pallas as pl
from jax.experimental.pallas import tpu as pltpu
from jax.sharding import PartitionSpec as P

HEAD = 128
THETA = 10000
SEQS, CACHE, D, FF, TP = 64, 4096, 3072, 8192, 8
QH = 3
HALF = D // 2
HID = FF // TP
SLOTS = 6
UNIT = 2
STEPS = SEQS // (2 * UNIT)
F32, BF16 = jnp.float32, jnp.bfloat16

GROUPS = (8,) * 8
PARTS = ((0, 1, 2, 3, 4, 5), (6,), (7,))
ROWS = [sum(GROUPS[g] for g in part) for part in PARTS]
CHUNKS = 6
EXCHANGES = [(None, g, rows, 0, HALF, g < 5) for g, rows in enumerate(GROUPS)]
EXCHANGES += [(0, 0, ROWS[0], i * (HALF // CHUNKS), HALF // CHUNKS, True) for i in range(CHUNKS)]
EXCHANGES += [(1, 6, ROWS[1], 0, HALF, True), (2, 7, ROWS[2], 0, HALF, False)]
A, B, C = len(GROUPS), len(GROUPS) + CHUNKS, len(GROUPS) + CHUNKS + 1


def after():
    plan = {k: [] for k in range(STEPS)}
    late = plan[STEPS - 1]
    for g in range(5):
        for lag, what in ((0, "wo"), (1, "share"), (3, "middle"), (5, "total"), (7, "forward")):
            k = 2 * g + 1 + lag
            if k < STEPS - 1:
                plan[k].append((what, g))
            else:
                late.append((46.05, what, g))
    for k, what, g in ((11, "wo", 5), (12, "load", 0), (12, "share", 5), (13, "middle", 5), (13, "wo", 6), (14, "share", 6)):
        plan[k].append((what, g))
    late += [(44.5, "wo", 7), (45.0, "middle", 6), (45.9, "total", 5), (46.0, "share", 7), (46.1, "normed", 0), (48.35, "middle", 7)]
    late += [(t, "wide", (0, j)) for j, t in enumerate((46.2, 46.9, 47.6, 48.4))]
    for i in range(CHUNKS):
        late += [(50.8 + 0.1 * i, "share", A + i), (53.5 + 1.07 * i, "middle", A + i)]
        late += [(56.3 + 1.07 * i, "total", A + i), (59.1 + 1.07 * i, "forward", A + i), (66.0 + 0.01 * i, "out", A + i)]
    late += [(49.1 + 0.6 * i, "down", A + 2 * i) for i in range(CHUNKS // 2)]
    late += [(50.4, "total", 6), (51.4, "normed", 1), (53.6, "total", 7), (53.61, "down", B), (54.7, "normed", 2), (55.6, "share", B)]
    late += [(51.5 + 0.53 * j, "wide", (1, j)) for j in range(4)] + [(54.8 + 0.53 * j, "wide", (2, j)) for j in range(4)]
    late += [(56.9, "down", C), (58.4, "middle", B), (58.5, "share", C), (61.2, "total", B), (61.25, "middle", C), (64.0, "forward", B)]
    late += [(65.7, "total", C), (66.1, "out", B), (67.0, "out", C)]
    plan[STEPS - 1] = [entry[1:] for entry in sorted(late, key=lambda entry: entry[0])]
    return {k: entries for k, entries in plan.items() if entries}


AFTER = after()


def rotary():
    half = HEAD // 2
    angle = np.float32(CACHE - 1) * np.float32(THETA) ** (-np.arange(half, dtype=np.float32) / np.float32(half))
    cos, sin = np.cos(angle), np.sin(angle)
    rows = [np.concatenate([cos, cos]), np.concatenate([-sin, sin])]
    return np.concatenate([np.stack(rows), np.zeros((6, HEAD))]).astype(np.float32)


def kernel(
    x_hbm, k_hbm, v_hbm, gain_a_hbm, gain_m_hbm, table_hbm, wq_hbm, wo_hbm, wg_hbm, wu_hbm, wd_hbm, y_ref,
    gains, gain_rows, table, wq, wo, wg, wu, wd, kbuf, vbuf, sbuf, obuf, qbuf, xs, states, hidden, sends, gots, mines, parts, nears, lefts, rights, halves,
    ksem, vsem, wsem, widesem, downsem, xsem, ssem, rsem,
):
    me = lax.axis_index("tp")
    z, c = me // 2, me % 2
    firsts = [sum(GROUPS[:g]) for g in range(len(GROUPS))]

    barrier = pltpu.get_barrier_semaphore()
    partner = 2 * z + (1 - c)
    near, across = lax.rem(3 * z + 1, 4), 3 - z
    outer = (z == 0) | (z == 3)
    inner = (z == 1) | (z == 2)
    for peer in (partner, *[2 * lax.rem(z + d, 4) + c for d in (1, 2, 3)]):
        pl.semaphore_signal(barrier, inc=1, device_id={"tp": peer}, device_id_type=pl.DeviceIdType.MESH)

    xcopies = [
        pltpu.make_async_copy(x_hbm.at[pl.ds(firsts[g], rows), pl.ds(i * HALF, HALF)], xs[g].at[i], xsem.at[g, i])
        for g, rows in enumerate(GROUPS)
        for i in range(2)
    ]
    small_copies = [
        pltpu.make_async_copy(gain_a_hbm, gains.at[0], wsem.at[5]),
        pltpu.make_async_copy(gain_m_hbm, gains.at[1], wsem.at[6]),
        pltpu.make_async_copy(table_hbm, table, wsem.at[7]),
    ]
    wcopies = [
        pltpu.make_async_copy(source, target, wsem.at[i])
        for i, (source, target) in enumerate([(wq_hbm, wq), (wo_hbm, wo)])
    ]
    tile, chunk = 256, HALF // CHUNKS

    def columns(source, target, first, width, sem):
        at = pl.ds(first, width)
        return pltpu.make_async_copy(source.at[:, at], target.at[:, at], sem)

    wide_copies = [
        [columns(source, target, j * tile, tile, widesem.at[j, i]) for i, (source, target) in enumerate([(wg_hbm, wg), (wu_hbm, wu)])]
        for j in range(HID // tile)
    ]
    down_copies = [[columns(wd_hbm, wd, i * HALF + j * chunk, chunk, downsem.at[j, i]) for i in range(2)] for j in range(CHUNKS)]

    def kcopy(p):
        slot = lax.rem(p, SLOTS)
        return pltpu.make_async_copy(k_hbm.at[pl.ds(2 * p, 2)], kbuf.at[slot], ksem.at[slot])

    def vcopy(p):
        slot = lax.rem(p, SLOTS)
        return pltpu.make_async_copy(v_hbm.at[pl.ds(2 * p, 2)], vbuf.at[slot], vsem.at[slot])

    for copy in (*xcopies, *small_copies, wcopies[0]):
        copy.start()
    for p in range(2):
        kcopy(p).start(priority=1)
        vcopy(p).start(priority=1)

    def normed(wide, gain):
        scale = lax.rsqrt(jnp.mean(wide * wide, -1, keepdims=True) + 1e-6)
        return (wide * scale * gain).astype(BF16)

    for copy in (*xcopies, *small_copies, wcopies[0]):
        copy.wait()
    for p in range(2, SLOTS):
        kcopy(p).start(priority=1)
        vcopy(p).start(priority=1)
    wcopies[1].start(priority=1)
    for i in range(2):
        for j in range(D // HEAD):
            gain_rows[i : i + 1, j * HEAD : (j + 1) * HEAD] = gains[i].astype(F32)[j : j + 1, :]
    wide = jnp.concatenate([jnp.concatenate([x[0].astype(F32), x[1].astype(F32)], 1) for x in xs], 0)
    q = jnp.dot(normed(wide, gain_rows[0:1, :]), wq[...], preferred_element_type=F32).astype(BF16).astype(F32)
    cos, sin = table[0:1, :], table[1:2, :]
    qbuf[...] = jnp.zeros_like(qbuf)
    for s in range(QH):
        t = q[:, s * HEAD : (s + 1) * HEAD]
        turned = t * cos + pltpu.roll(t, HEAD // 2, 1) * sin
        qbuf[:, s, :] = turned.astype(BF16).astype(F32)

    def scores(p):
        slot, kept = lax.rem(p, SLOTS), lax.rem(p, 2 * UNIT)
        first = qbuf[2 * p]
        second = pltpu.roll(qbuf[2 * p + 1], QH, 0)
        row = lax.broadcasted_iota(jnp.int32, first.shape, 0)
        second = jnp.where((row >= QH) & (row < 2 * QH), second, 0.0)
        both = jnp.concatenate([first, second], 1).astype(BF16)
        for i in range(CACHE // tile):
            at = pl.ds(i * tile, tile)
            keys = jnp.concatenate([kbuf[slot, 0, at, :], kbuf[slot, 1, at, :]], 1)
            found = lax.dot_general(both, keys, (((1,), (1,)), ((), ())), preferred_element_type=F32)
            sbuf[kept, :, at] = found * HEAD**-0.5

    def finish(p):
        slot, kept = lax.rem(p, SLOTS), lax.rem(p, 2 * UNIT)
        s = sbuf[kept]
        e = jnp.exp(s - jnp.max(s, -1, keepdims=True))
        w = (e * (1.0 / jnp.sum(e, -1, keepdims=True))).astype(BF16)
        sums = [None, None]
        for i in range(CACHE // tile):
            at = pl.ds(i * tile, tile)
            values = jnp.concatenate([vbuf[slot, 0, at, :], vbuf[slot, 1, at, :]], 1)
            term = jnp.dot(w[:, i * tile : (i + 1) * tile], values, preferred_element_type=F32)
            sums[i % 2] = term if sums[i % 2] is None else sums[i % 2] + term
        for i, total in enumerate(sums):
            obuf[i, pl.ds(pl.multiple_of(16 * p, 16), 8), :] = total[:, :HEAD]
            obuf[i, pl.ds(pl.multiple_of(16 * p + 8, 8), 8), :] = pltpu.roll(total[:, HEAD:], 8 - QH, 0)

    def step(k, last):
        for u in range(UNIT):
            vcopy(k * UNIT + u).wait()
            if not last:
                kcopy((k + 1) * UNIT + u).wait()
        for u in range(UNIT):
            finish(k * UNIT + u)
        if last:
            return
        for u in range(UNIT):
            scores((k + 1) * UNIT + u)
        for u in range(UNIT):
            for copy, p in ((vcopy, k * UNIT + u), (kcopy, (k + 1) * UNIT + u)):

                @pl.when(p + SLOTS < SEQS // 2)
                def _():
                    copy(p + SLOTS).start(priority=1)

    def remote(e, i, source, target, peer):
        return pltpu.make_async_remote_copy(
            src_ref=source,
            dst_ref=target,
            send_sem=ssem.at[e, i],
            recv_sem=rsem.at[e, i],
            device_id={"tp": peer},
            device_id_type=pl.DeviceIdType.MESH,
        )

    def to_partner(e):
        return remote(e, 0, sends[e], gots[e], partner)

    def to_inner(e):
        return remote(e, 1, parts[e], nears[e], 2 * near + c)

    def two_chips(e):
        targets = [(rights, across), (rights, 3 - near), (lefts, near)]
        return [remote(e, 2 + i, parts[e], refs[e], 2 * chip + c) for i, (refs, chip) in enumerate(targets[: 1 if EXCHANGES[e][5] else 3])]

    def finished(e):
        return remote(e, 5, halves[e].at[c], halves[e].at[c], 2 * near + c)

    def halves_to_partner(e):
        return remote(e, 6, halves[e].at[c], halves[e].at[c], partner)

    def terms(exchanges, left, right_ref):
        first, columns = EXCHANGES[exchanges[0]][3:5]
        width = 512
        for mine in (False, True):
            base = (c if mine else 1 - c) * HALF + first
            for j in range(0, columns * len(exchanges), width):
                at = pl.ds(pl.multiple_of(base + j, 256), width)
                term = jnp.dot(left, right_ref[:, at], preferred_element_type=F32)
                for i in range(0, width, min(width, columns)):
                    e, to = exchanges[(j + i) // columns], (j + i) % columns
                    piece = term[:, i : i + min(width, columns)]
                    if mine:
                        mines[e][:, to : to + piece.shape[1]] = piece
                    else:
                        sends[e][:, to : to + piece.shape[1]] = piece.astype(BF16)
            if not mine:
                for e in exchanges:
                    to_partner(e).start()

    def share(e):
        to_partner(e).wait()
        total = mines[e][...] + gots[e][...].astype(F32)
        mines[e][...] = total
        parts[e][...] = total.astype(BF16)

        @pl.when(outer)
        def _():
            to_inner(e).start()

    def middle(e):
        @pl.when(inner)
        def _():
            to_inner(e).wait_recv()
            parts[e][...] = (mines[e][...] + nears[e][...].astype(F32)).astype(BF16)
            for copy in two_chips(e):
                copy.start()

    def base_of(e):
        part, g, _, first, columns, _ = EXCHANGES[e]
        if part is None:
            return xs[g][c].astype(F32)
        return jnp.concatenate([halves[g][c, :, first : first + columns].astype(F32) for g in PARTS[part]], 0)

    def total(e):
        copies = two_chips(e)

        def finish_with(ref):
            both = ref[...].astype(F32) + rights[e][...].astype(F32)
            halves[e][c] = (base_of(e) + both).astype(BF16)
            halves_to_partner(e).start()

        @pl.when(inner)
        def _():
            copies[0].wait_recv()
            finish_with(parts[e])
            if EXCHANGES[e][5]:
                finished(e).start()

        if not EXCHANGES[e][5]:

            @pl.when(outer)
            def _():
                copies[2].wait_recv()
                copies[1].wait_recv()
                finish_with(lefts[e])

    def forward(e):
        @pl.when(outer)
        def _():
            finished(e).wait_recv()
            halves_to_partner(e).start()

    def sent(e):
        @pl.when(outer)
        def _():
            to_inner(e).wait_send()

        @pl.when(inner)
        def _():
            for copy in two_chips(e):
                copy.wait_send()
            if EXCHANGES[e][5]:
                finished(e).wait_send()

    def normed_states(part):
        groups = PARTS[part]
        for g in groups:
            halves_to_partner(g).wait()
            sent(g)
        h = jnp.concatenate([jnp.concatenate([halves[g][i].astype(F32) for i in range(2)], 1) for g in groups], 0)
        states[part][...] = normed(h, gain_rows[1:2, :])

    def wide_part(part, j):
        if part == 0:
            for copy in wide_copies[j]:
                copy.wait()
        at = pl.ds(j * tile, tile)
        gate = jnp.dot(states[part][...], wg[:, at], preferred_element_type=F32)
        up = jnp.dot(states[part][...], wu[:, at], preferred_element_type=F32)
        hidden[part][:, at] = (jax.nn.silu(gate) * up).astype(BF16)

    started = set()

    def do(what, e):
        if what == "wo":
            if not started:
                pl.semaphore_wait(barrier, 4)
                wcopies[1].wait()
            started.add("wo")
            seen = []
            for s in range(QH):
                at = pl.ds(8 * firsts[e] + s, GROUPS[e], stride=8)
                seen.append(obuf[0, at, :] + obuf[1, at, :])
            terms([e], jnp.concatenate(seen, 1).astype(BF16), wo)
        elif what == "load":
            for copies in (*wide_copies, *down_copies):
                for copy in copies:
                    copy.start(priority=1)
        elif what == "share":
            share(e)
        elif what == "middle":
            middle(e)
        elif what == "total":
            total(e)
        elif what == "normed":
            normed_states(e)
        elif what == "wide":
            wide_part(*e)
        elif what == "down":
            part = EXCHANGES[e][0]
            exchanges = [e, e + 1] if part == 0 else [e]
            if part == 0:
                for i in exchanges:
                    for copy in down_copies[i - A]:
                        copy.wait()
            terms(exchanges, hidden[part][...], wd)
        elif what == "forward":
            forward(e)
        elif what == "out":
            halves_to_partner(e).wait()
            sent(e)
            _, g, rows, first, columns, _ = EXCHANGES[e]
            for i in range(2):
                y_ref[firsts[g] : firsts[g] + rows, i * HALF + first : i * HALF + first + columns] = halves[e][i]

    for u in range(UNIT):
        kcopy(u).wait()
        scores(u)
        kcopy(u + SLOTS).start(priority=1)
    at = 0
    for k in sorted(AFTER):
        if k < STEPS - 1:
            lax.fori_loop(at, k + 1, lambda i, _: step(i, False), None)
        else:
            if at < STEPS - 1:
                lax.fori_loop(at, STEPS - 1, lambda i, _: step(i, False), None)
            step(STEPS - 1, True)
        at = k + 1
        for what, e in AFTER[k]:
            do(what, e)


def layer(x, k, v, gain_a, gain_m, table, wq, wo, wg, wu, wd):
    n = len(EXCHANGES)
    each = lambda *lead, dtype=BF16: [pltpu.VMEM((*lead, rows, width), dtype) for _, _, rows, _, width, _ in EXCHANGES]
    parts = lambda width: [pltpu.VMEM((rows, width), BF16) for rows in ROWS]
    return pl.pallas_call(
        kernel,
        out_shape=jax.ShapeDtypeStruct((SEQS, D), BF16),
        in_specs=[pl.BlockSpec(memory_space=pltpu.HBM)] * 11,
        out_specs=pl.BlockSpec(memory_space=pltpu.VMEM),
        scratch_shapes=[
            pltpu.VMEM((2, *gain_a.shape), BF16),
            pltpu.VMEM((2, D), F32),
            pltpu.VMEM(table.shape, F32),
            pltpu.VMEM(wq.shape, BF16),
            pltpu.VMEM(wo.shape, BF16),
            pltpu.VMEM(wg.shape, BF16),
            pltpu.VMEM(wu.shape, BF16),
            pltpu.VMEM(wd.shape, BF16),
            pltpu.VMEM((SLOTS, 2, CACHE, HEAD), BF16),
            pltpu.VMEM((SLOTS, 2, CACHE, HEAD), BF16),
            pltpu.VMEM((2 * UNIT, 8, CACHE), F32),
            pltpu.VMEM((2, SEQS * 8, HEAD), F32),
            pltpu.VMEM((SEQS, 8, HEAD), F32),
            [pltpu.VMEM((2, rows, HALF), BF16) for rows in GROUPS],
            parts(D),
            parts(HID),
            each(),
            each(),
            each(dtype=F32),
            each(),
            each(),
            each(),
            each(),
            each(2),
            pltpu.SemaphoreType.DMA((SLOTS,)),
            pltpu.SemaphoreType.DMA((SLOTS,)),
            pltpu.SemaphoreType.DMA((8,)),
            pltpu.SemaphoreType.DMA((HID // 256, 2)),
            pltpu.SemaphoreType.DMA((CHUNKS, 2)),
            pltpu.SemaphoreType.DMA((len(GROUPS), 2)),
            pltpu.SemaphoreType.DMA((n, 7)),
            pltpu.SemaphoreType.DMA((n, 7)),
        ],
        compiler_params=pltpu.CompilerParams(collective_id=0, has_side_effects=True, vmem_limit_bytes=63 * 2**20),
    )(x, k, v, gain_a, gain_m, table, wq, wo, wg, wu, wd)


def solution(mesh):
    table = rotary()

    def step(x, k_cache, v_cache, gain_a, wq, wo, gain_m, w_gate, w_up, w_down):
        seqs, cache = k_cache.shape[:2]
        k, v = (t.reshape(seqs, cache, HEAD) for t in (k_cache, v_cache))
        gain_a, gain_m = (t.reshape(-1, HEAD) for t in (gain_a, gain_m))
        return layer(x, k, v, gain_a, gain_m, jnp.asarray(table), wq, wo, w_gate, w_up, w_down)

    states, cache, columns, rows_of = P("dp", None), P("dp", None, "tp", None), P(None, "tp"), P("tp", None)
    return jax.shard_map(
        step,
        mesh=mesh,
        in_specs=(states, cache, cache, P(None), columns, rows_of, P(None), columns, columns, rows_of),
        out_specs=states,
        check_vma=False,
    )
```

time: 84.2 us -> 74.7 us (0.89)
  Pallas kernels: 79.3 us -> 72.7 us
  other arithmetic: 2.78 us -> 0 us
    pallas_call x1, Pallas kernels: 79.3 us -> 72.7 us  [layer(): pl.pallas_call(kernel, out_shape=jax.ShapeDtypeStruct((SEQS, D), BF16), i...]
    another operation x3 -> x0, other arithmetic: 2.78 us -> none  [step(): jnp.stack([gain_a.astype(F32), gain_m.astype(F32), pad(cos), pad(sin)])]
where the time goes in v2:
time: 74.7 us; the launch traced here: 74.5 us
  Pallas kernels  72.7 us (97%)
  local copies, waits for them, and re-layouts  1.77 us (2%)
    pallas_call x1, Pallas kernels, layer(): pl.pallas_call(kernel, out_shape=jax.ShapeDtypeStruct((SEQS, D), BF16), i...  72.7 us
    unnamed x1, local copies, waits for them, and re-layouts  1.77 us

profile of v2, /device:TPU:0, one launch (start us, length us, event | category | flops | bytes accessed | tf_op | source)
XLA Modules:
  0.0 74.5 jit_solution(2060660410529281976)
XLA Ops:
  0.0 72.7 %shard_map.109 = bf16[64,3072]{1,0:T(8,128)(2,1)} custom-call(bf16[64,3072]{1,0:T(8,128)(2,1)} %x_hbm.1, bf16[64,4096,128]{2,1,0:T(8,128)(2,1)} %bitcast.k_hbm, bf16[64,4096,128]{2,1,0:T(8,128)(2,1)} %bitcast.1.v_hbm, bf16[24,128]{1,0:T(8,128)(2,1)} %bitcast.4, bf16[24,128]{1,0:T(8,128)(2,1)} %bitcast.5, f32[8,128]{1,0:T(8,128)} %constant.2.clone.table_hbm, ...), custom_call_target="tpu_custom_call" | custom-call | tf_op jit(solution)/shard_map/pallas_call | solution.py:384
  72.8 1.8 %copy.13 = bf16[64,3072]{1,0:T(8,128)(2,1)} copy(bf16[64,3072]{1,0:T(8,128)(2,1)} %shard_map.109) | data formatting | bytes 786432

commit v3 on v2

--- a/solution.py
+++ b/solution.py
@@ -42,12 +42,12 @@
     late += [(44.5, "wo", 7), (45.0, "middle", 6), (45.9, "total", 5), (46.0, "share", 7), (46.1, "normed", 0), (48.35, "middle", 7)]
     late += [(t, "wide", (0, j)) for j, t in enumerate((46.2, 46.9, 47.6, 48.4))]
     for i in range(CHUNKS):
-        late += [(50.8 + 0.1 * i, "share", A + i), (53.5 + 1.07 * i, "middle", A + i)]
-        late += [(56.3 + 1.07 * i, "total", A + i), (59.1 + 1.07 * i, "forward", A + i), (66.0 + 0.01 * i, "out", A + i)]
+        late += [((50.8 if i < 4 else 51.6) + 0.1 * i, "share", A + i), ((53.5 + 1.07 * i) if i < 4 else 57.0 + 0.01 * i, "middle", A + i)]
+        late += [(57.2 + 0.05 * i, "total", A + i), (59.1 + 1.07 * i, "forward", A + i), (66.0 + 0.01 * i, "out", A + i)]
     late += [(49.1 + 0.6 * i, "down", A + 2 * i) for i in range(CHUNKS // 2)]
     late += [(50.4, "total", 6), (51.4, "normed", 1), (53.6, "total", 7), (53.61, "down", B), (54.7, "normed", 2), (55.6, "share", B)]
-    late += [(51.5 + 0.53 * j, "wide", (1, j)) for j in range(4)] + [(54.8 + 0.53 * j, "wide", (2, j)) for j in range(4)]
-    late += [(56.9, "down", C), (58.4, "middle", B), (58.5, "share", C), (61.2, "total", B), (61.25, "middle", C), (64.0, "forward", B)]
+    late += [(51.5 + 1.06 * j, "wide", (1, j)) for j in range(2)] + [(54.8 + 1.06 * j, "wide", (2, j)) for j in range(2)]
+    late += [(56.9, "down", C), (57.0, "share", C), (57.15, "middle", B), (57.36, "middle", C), (57.42, "total", B), (64.0, "forward", B)]
     late += [(65.7, "total", C), (66.1, "out", B), (67.0, "out", C)]
     plan[STEPS - 1] = [entry[1:] for entry in sorted(late, key=lambda entry: entry[0])]
     return {k: entries for k, entries in plan.items() if entries}
@@ -65,9 +65,9 @@
 
 
 def kernel(
-    x_hbm, k_hbm, v_hbm, gain_a_hbm, gain_m_hbm, table_hbm, wq_hbm, wo_hbm, wg_hbm, wu_hbm, wd_hbm, y_ref,
+    x_hbm, k_hbm, v_hbm, gain_a_hbm, gain_m_hbm, table_hbm, wq_hbm, wo_hbm, wg_hbm, wu_hbm, wd_hbm, y_hbm,
     gains, gain_rows, table, wq, wo, wg, wu, wd, kbuf, vbuf, sbuf, obuf, qbuf, xs, states, hidden, sends, gots, mines, parts, nears, lefts, rights, halves,
-    ksem, vsem, wsem, widesem, downsem, xsem, ssem, rsem,
+    ksem, vsem, wsem, widesem, downsem, xsem, ysem, ssem, rsem,
 ):
     me = lax.axis_index("tp")
     z, c = me // 2, me % 2
@@ -311,7 +311,8 @@
         if part == 0:
             for copy in wide_copies[j]:
                 copy.wait()
-        at = pl.ds(j * tile, tile)
+        width = tile if part == 0 else HID // 2
+        at = pl.ds(j * width, width)
         gate = jnp.dot(states[part][...], wg[:, at], preferred_element_type=F32)
         up = jnp.dot(states[part][...], wu[:, at], preferred_element_type=F32)
         hidden[part][:, at] = (jax.nn.silu(gate) * up).astype(BF16)
@@ -356,9 +357,17 @@
         elif what == "out":
             halves_to_partner(e).wait()
             sent(e)
-            _, g, rows, first, columns, _ = EXCHANGES[e]
-            for i in range(2):
-                y_ref[firsts[g] : firsts[g] + rows, i * HALF + first : i * HALF + first + columns] = halves[e][i]
+            for copy in ycopies(e):
+                copy.start()
+
+    def ycopies(e):
+        _, g, rows, first, columns, _ = EXCHANGES[e]
+        return [
+            pltpu.make_async_copy(
+                halves[e].at[i], y_hbm.at[pl.ds(firsts[g], rows), pl.ds(i * HALF + first, columns)], ysem.at[e - A, i]
+            )
+            for i in range(2)
+        ]
 
     for u in range(UNIT):
         kcopy(u).wait()
@@ -375,6 +384,9 @@
         at = k + 1
         for what, e in AFTER[k]:
             do(what, e)
+    for e in range(A, len(EXCHANGES)):
+        for copy in ycopies(e):
+            copy.wait()
 
 
 def layer(x, k, v, gain_a, gain_m, table, wq, wo, wg, wu, wd):
@@ -385,7 +397,7 @@
         kernel,
         out_shape=jax.ShapeDtypeStruct((SEQS, D), BF16),
         in_specs=[pl.BlockSpec(memory_space=pltpu.HBM)] * 11,
-        out_specs=pl.BlockSpec(memory_space=pltpu.VMEM),
+        out_specs=pl.BlockSpec(memory_space=pltpu.HBM),
         scratch_shapes=[
             pltpu.VMEM((2, *gain_a.shape), BF16),
             pltpu.VMEM((2, D), F32),
@@ -417,6 +429,7 @@
             pltpu.SemaphoreType.DMA((HID // 256, 2)),
             pltpu.SemaphoreType.DMA((CHUNKS, 2)),
             pltpu.SemaphoreType.DMA((len(GROUPS), 2)),
+            pltpu.SemaphoreType.DMA((n - A, 2)),
             pltpu.SemaphoreType.DMA((n, 7)),
             pltpu.SemaphoreType.DMA((n, 7)),
         ],

time: 74.7 us -> 74.6 us (level)
  no operation moved by 1% of the time
where the time goes in v3:
time: 74.6 us; the launch traced here: 74.4 us
  Pallas kernels  72.7 us (97%)
  local copies, waits for them, and re-layouts  1.77 us (2%)
    pallas_call x1, Pallas kernels, layer(): pl.pallas_call(kernel, out_shape=jax.ShapeDtypeStruct((SEQS, D), BF16), i...  72.7 us
    unnamed x1, local copies, waits for them, and re-layouts  1.77 us

profile of v3, /device:TPU:0, one launch (start us, length us, event | category | flops | bytes accessed | tf_op | source)
XLA Modules:
  0.0 74.4 jit_solution(8045984305339717136)
XLA Ops:
  0.0 72.7 %shard_map.109 = bf16[64,3072]{1,0:T(8,128)(2,1)} custom-call(bf16[64,3072]{1,0:T(8,128)(2,1)} %x_hbm.1, bf16[64,4096,128]{2,1,0:T(8,128)(2,1)} %bitcast.k_hbm, bf16[64,4096,128]{2,1,0:T(8,128)(2,1)} %bitcast.1.v_hbm, bf16[24,128]{1,0:T(8,128)(2,1)} %bitcast.4, bf16[24,128]{1,0:T(8,128)(2,1)} %bitcast.5, f32[8,128]{1,0:T(8,128)} %constant.2.clone.table_hbm, ...), custom_call_target="tpu_custom_call" | custom-call | tf_op jit(solution)/shard_map/pallas_call | solution.py:396
  72.7 1.8 %copy.13 = bf16[64,3072]{1,0:T(8,128)(2,1)} copy(bf16[64,3072]{1,0:T(8,128)(2,1)} %shard_map.109) | data formatting | bytes 786432
